TPU v7x, 256 devices: a whole 4x4x8 slice. The times are simulated.
256 devices in a mesh: tm: 128 (over x, y_hi, z, core), chan: 2 (over y_lo).
Axes of the slice: x: 4, y: 4 (y_hi: 2, y_lo: 2; y = y_hi * 2 + y_lo), z: 8, core: 2. Of those that a mesh axis runs over, the one named last changes fastest.
Arguments:
- random_forcing: bfloat16 [49152, 4096], P('tm', 'chan'), may hold values from -6 to 6
- eigen_root_table: float32 [768, 4096], P(None, 'chan'), may hold values from 0.1 to 2
- lane_fading_speed: float32 [4096], P('chan'), may hold values from 4.0690104e-08 to 0.025, as said below
- sudden_shrink: float32 [49152], P('tm'), may hold values from 0.125 to 1, as said below
Outputs:
- sample: float32 [49152, 4096], P('tm', 'chan')
Inputs may be any that keep to these rules, and one draw needn't show every extreme that they name: `lane_fading_speed`: every channel's rate is positive. `sudden_shrink`: every entry lies in (0, 1], and the product of all entries is at most 0.52.
All inputs are finite; a program needn't handle non-finite values.
Results may differ from a plain program's by a relative error of at most 0.0003.
Values may be sent and summed in bfloat16 or wider, within the bound.
A program may use at most 192 MiB of HBM per device.

v0:
```python
import jax
import jax.numpy as jnp
from jax import lax
from jax.sharding import Mesh
from jax.sharding import PartitionSpec as P

TM = ("tm_0", "tm_1", "tm_2", "tm_3")


def from_behind(value, axis, steps):
    count = lax.axis_size(axis)
    pairs = [(source, (source + steps) % count) for source in range(count)]
    return lax.ppermute(value, axis, pairs)


def filled_with(array, identity):
    return jax.tree.map(
        lambda a, e: jnp.broadcast_to(jnp.asarray(e, a.dtype), a.shape), array, identity
    )


def collected_together(array, axis):
    leaves = jax.tree.leaves(array)
    order = sorted(range(len(leaves)), key=lambda k: -leaves[k].size)
    width = (1, *leaves[order[0]].shape)[-1]
    lines = [
        jnp.pad(leaves[k].reshape(-1), (0, -leaves[k].size % width)).reshape(-1, width)
        for k in order
    ]
    both, at, found = (lax.all_gather(jnp.concatenate(lines), axis), 0, {})
    for k, line in zip(order, lines):
        slab = both[:, at : at + len(line)].reshape(len(both), -1)
        found[k] = slab[:, : leaves[k].size].reshape(-1, *leaves[k].shape)
        at += len(line)
    numbers = iter(range(len(leaves)))
    return jax.tree.map(lambda _: found[next(numbers)], array)


def carried_in(array, axes, combine, identity):
    before = start = filled_with(array, identity)
    so_far = array
    for axis in reversed(axes):
        peers, position = (lax.axis_size(axis), lax.axis_index(axis))
        pieces = collected_together(so_far, axis)
        inside, so_far = (start, start)
        for k in range(peers):
            passed = k < position
            so_far = combine(so_far, jax.tree.map(lambda part: part[k], pieces))
            inside = jax.tree.map(lambda new, old: jnp.where(passed, new, old), so_far, inside)
        before = combine(inside, before)
    return before


def from_root(array, axes, root):
    array = jnp.where(lax.axis_index(axes) == root, array, jnp.zeros_like(array))
    for axis in axes:
        array = lax.psum(array, axis)
    return array


def combine(former, latter):
    return (former[0] + latter[0], jnp.exp(latter[0]) * former[1] + latter[1])


def tables(length):
    indices = jnp.arange(2 * length, dtype=jnp.int32)
    product = indices[:, None] * indices[None, :] % (2 * length)
    angles = product.astype(jnp.float32) * (jnp.pi / length)
    cosine = jnp.cos(angles)
    sine_table = jnp.sin(angles)
    forward = jnp.concatenate([cosine[:, :length], -sine_table[:, :length]], axis=0)
    inverse = jnp.concatenate([cosine, -sine_table], axis=1) / (2.0 * length)
    return (forward, inverse)


def spectra(segment, forward, spectrum, length):
    values = jnp.dot(
        forward,
        segment.astype(jnp.float32),
        precision=lax.Precision.HIGHEST,
        preferred_element_type=jnp.float32,
    )
    return jnp.concatenate(
        [spectrum * values[: 2 * length], spectrum * values[2 * length :]], axis=0
    )


def invert(scaled, inverse, first, count):
    return jnp.dot(
        inverse[first : first + count],
        scaled,
        precision=lax.Precision.HIGHEST,
        preferred_element_type=jnp.float32,
    )


def shards(random_forcing, eigen_root_table, lane_fading_speed, sudden_shrink):
    length = random_forcing.shape[0]
    width = random_forcing.shape[1]
    forward, inverse = tables(length)
    earlier_noise = from_behind(random_forcing, TM, 1)
    stacked = jnp.concatenate([random_forcing, earlier_noise], axis=1)
    doubled = jnp.concatenate([eigen_root_table, eigen_root_table], axis=1)
    scaled = spectra(stacked, forward, doubled, length)
    own_part = invert(scaled[:, :width], inverse, 0, length)
    earlier_part = invert(scaled[:, width:], inverse, length, length)
    noise_sequence = own_part + earlier_part
    tick_log_growth = jnp.log(sudden_shrink)[:, None] - lane_fading_speed[None, :]
    power_entries = (sudden_shrink * sudden_shrink)[:, None]
    weights = jnp.sqrt(
        1.0 - power_entries + power_entries * (-jnp.expm1(-2.0 * lane_fading_speed))[None, :]
    )
    rows = jnp.arange(length, dtype=jnp.int32)
    lower = (rows[:, None] >= rows[None, :]).astype(jnp.float32)
    logs = jnp.dot(
        lower, tick_log_growth, precision=lax.Precision.HIGHEST, preferred_element_type=jnp.float32
    )
    rescaled = jnp.exp(-logs) * (weights * noise_sequence)
    states = jnp.exp(logs) * jnp.dot(
        lower, rescaled, precision=lax.Precision.HIGHEST, preferred_element_type=jnp.float32
    )
    own_total = (logs[-1], states[-1])
    zeroes = jnp.zeros_like(own_total[0])
    preceding_input = carried_in(own_total, TM, combine, (zeroes, zeroes))
    through = combine(preceding_input, own_total)
    entire = (
        from_root(through[0], TM, lax.axis_size(TM) - 1),
        from_root(through[1], TM, lax.axis_size(TM) - 1),
    )
    opening = entire[1] / -jnp.expm1(entire[0])
    incoming = jnp.exp(preceding_input[0]) * opening + preceding_input[1]
    return states + jnp.exp(logs) * incoming[None, :]


def solution(mesh):
    torus = Mesh(
        mesh.devices.reshape(4, 2, 8, 2, mesh.shape["chan"]),
        ("tm_0", "tm_1", "tm_2", "tm_3", "chan"),
    )
    return jax.shard_map(
        shards,
        mesh=torus,
        in_specs=(P(TM, "chan"), P(None, "chan"), P("chan"), P(TM)),
        out_specs=P(TM, "chan"),
        check_vma=False,
    )
```

profile of v0, /device:TPU:1, one launch (start us, length us, event | category | flops | bytes accessed | tf_op | source)
XLA Modules:
  0.0 237.6 jit_solution(13609140888398446958)
XLA Ops:
  0.0 3.0 %collective-permute-start = (bf16[384,2048]{1,0:T(8,128)(2,1)}, bf16[384,2048]{1,0:T(8,128)(2,1)}, u32[]{:S(2)}, u32[]{:S(2)}) collective-permute-start(bf16[384,2048]{1,0:T(8,128)(2,1)} %param.4), channel_id=1, source_target_pairs={{0,2},{2,4},{4,6},{6,8},{8,10},{10,12},{12,14},{14,16},{16,18},{18... | collective-permute-start | bytes 4718600 | tf_op jit(solution)/shard_map/ppermute | solution.py:13
  3.0 10.5 %fusion.32 = (f32[768,768]{1,0:T(8,128)S(1)}, f32[768,768]{1,0:T(8,128)}) fusion(), kind=kLoop, calls=%fused_computation.39 | loop fusion | flops 5898240 | bytes 4718592 | tf_op jit(solution)/shard_map/cos | solution.py:69
  13.5 0.1 slice.241
  13.6 0.0 copy-done.12
  13.6 0.6 broadcast_subtract_fusion
  14.2 0.0 copy-done.11
  14.2 2.9 %fusion.18 = f32[384,2048]{1,0:T(8,128)S(1)} fusion(f32[2048]{0:T(1024)S(1)} %copy-done.11, f32[384]{0:T(512)S(1)} %get-tuple-element.39), kind=kOutput, calls=%fused_computation.25 | convolution fusion | flops 3624812544 | bytes 3155456 | tf_op jit(solution)/shard_map/dot_general | solution.py:115
  17.1 0.0 copy-start.3
  17.1 1.7 copy-done.3
  18.8 9.1 %fusion.31 = f32[768,768]{1,0:T(8,128)S(1)} fusion(), kind=kLoop, calls=%fused_computation.38 | loop fusion | flops 5308416 | bytes 2359296 | tf_op jit(solution)/shard_map/sin | solution.py:70
  27.9 0.0 slice-start
  27.9 0.1 slice_negate_fusion
  28.0 0.0 slice-start.1
  28.0 3.4 %constant_dynamic-update-slice_fusion.1 = f32[768,4096]{1,0:T(8,128)S(1)} fusion(f32[768,2048]{1,0:T(8,128)} %param.5), kind=kLoop, calls=%fused_computation.112 | loop fusion | bytes 12582912
  31.4 0.5 slice-done
  31.9 0.7 slice-done.1
  32.6 0.8 constant_dynamic-update-slice_fusion
  33.4 0.0 copy-start.1
  33.4 0.9 copy-done.7
  34.3 2.8 %maximum_multiply_fusion = f32[768,1536]{1,0:T(8,128)} fusion(f32[768,768]{1,0:T(8,128)S(1)} %copy-done.7, f32[768,768]{1,0:T(8,128)S(1)} %get-tuple-element.40), kind=kLoop, calls=%fused_computation.9 | loop fusion | flops 2359296 | bytes 9437184 | tf_op jit(solution)/shard_map/div | solution.py:72
  37.1 0.0 collective-permute-done
  37.1 2.5 %copy-done.1 = f32[768,4096]{1,0:T(8,128)} copy-done((f32[768,4096]{1,0:T(8,128)}, f32[768,4096]{1,0:T(8,128)S(1)}, u32[]{:S(2)}) %copy-start.1) | copy-done | bytes 12582936
  39.6 0.0 copy-done.8
  39.6 23.3 %fusion.5 = f32[1536,4096]{1,0:T(8,128)} fusion(bf16[384,2048]{1,0:T(8,128)(2,1)} %collective-permute-done, bf16[384,2048]{1,0:T(8,128)(2,1)S(1)} %copy-done.8, f32[768,384]{1,0:T(8,128)S(1)} %slice_negate_fusion, f32[768,384]{1,0:T(8,128)S(1)} %slice.241), kind=kOutput, calls=%fused_computation.11 | convolution fusion | flops 28997910528 | bytes 30670848 | tf_op jit(solution)/shard_map/dot_general | solution.py:77
  62.9 18.3 %slice_multiply_fusion = (f32[768,4096]{1,0:T(8,128)S(1)}, f32[768,4096]{1,0:T(8,128)}) fusion(f32[768,4096]{1,0:T(8,128)} %copy-done.1, f32[1536,4096]{1,0:T(8,128)} %fusion.5), kind=kLoop, calls=%fused_computation.7 | loop fusion | flops 6291456 | bytes 62914560 | tf_op jit(solution)/shard_map/mul | solution.py:84
  81.3 19.2 %fusion.3 = f32[384,2048]{1,0:T(8,128)} fusion(f32[768,4096]{1,0:T(8,128)S(1)} %get-tuple-element.28, f32[768,4096]{1,0:T(8,128)} %get-tuple-element.29, f32[768,1536]{1,0:T(8,128)} %maximum_multiply_fusion), kind=kOutput, calls=%fused_computation.5 | convolution fusion | flops 14498660352 | bytes 30670848 | tf_op jit(solution)/shard_map/dot_general | solution.py:89
  100.4 0.0 copy-done
  100.5 0.0 copy-done.2
  100.5 0.0 copy-start.9
  100.5 0.0 copy-start.10
  100.5 17.2 %fusion.1 = f32[384,2048]{1,0:T(8,128)} fusion(f32[768,4096]{1,0:T(8,128)S(1)} %copy-done, f32[768,4096]{1,0:T(8,128)S(1)} %get-tuple-element.28, f32[768,1536]{1,0:T(8,128)S(1)} %copy-done.2), kind=kOutput, calls=%fused_computation.3 | convolution fusion | flops 14498660352 | bytes 30670848 | tf_op jit(solution)/shard_map/dot_general | solution.py:89
  117.7 0.0 copy-done.4
  117.7 0.0 copy-start.5
  117.7 6.5 %exponential_multiply_fusion = f32[384,2048]{1,0:T(8,128)S(1)} fusion(f32[384,2048]{1,0:T(8,128)S(1)} %copy-done.4, f32[384,2048]{1,0:T(8,128)} %fusion.1, f32[384,2048]{1,0:T(8,128)} %fusion.3, f32[2048]{0:T(1024)S(1)} %exponential-minus-one_negate_fusion, f32[384]{0:T(512)S(1)} %copy-done.10, f32[384]{0:T(512)S(1)} %copy-done.9), kind=kOutput, calls=%fused_computation.27 | convolution fusion | flops 3629531136 | bytes 12594176 | tf_op jit(solution)/shard_map/dot_general | solution.py:119
  124.2 1.6 copy-done.6
  125.9 1.8 all-gather.4
  127.8 21.2 %all-gather.5 = f32[8,2,2048]{2,1,0:T(2,128)S(1)} all-gather(f32[1,2,2048]{2,1,0:T(2,128)S(1)} %maximum_bitcast_fusion.1), channel_id=3, replica_groups=mesh['tm_0'=4,'tm_1'=2,'tm_2'=8,'tm_3'=2,'chan'=2] {'tm_2'}, dimensions={0}, use_global_device_ids=true | all-gather | bytes 147456 | tf_op jit(solution)/shard_map/all_gather | solution.py:30
  149.0 0.1 fusion.46
  149.1 0.1 broadcast_select_fusion.1
  149.3 4.8 %all-gather.6 = f32[2,2,2048]{2,1,0:T(2,128)S(1)} all-gather(f32[1,2,2048]{2,1,0:T(2,128)S(1)} %maximum_bitcast_fusion.2), channel_id=4, replica_groups=mesh['tm_0'=4,'tm_1'=2,'tm_2'=8,'tm_3'=2,'chan'=2] {'tm_1'}, dimensions={0}, use_global_device_ids=true | all-gather | bytes 49152 | tf_op jit(solution)/shard_map/all_gather | solution.py:30
  154.1 9.3 %all-gather.7 = f32[4,2,2048]{2,1,0:T(2,128)S(1)} all-gather(f32[1,2,2048]{2,1,0:T(2,128)S(1)} %maximum_bitcast_fusion.3), channel_id=5, replica_groups=mesh['tm_0'=4,'tm_1'=2,'tm_2'=8,'tm_3'=2,'chan'=2] {'tm_0'}, dimensions={0}, use_global_device_ids=true | all-gather | bytes 81920 | tf_op jit(solution)/shard_map/all_gather | solution.py:30
  163.4 0.1 fusion.40
  163.5 0.1 fusion.41
  163.7 12.8 %all-reduce.1 = (f32[2048]{0:T(1024)S(1)}, f32[2048]{0:T(1024)S(1)}) all-reduce(f32[2048]{0:T(1024)S(1)} %get-tuple-element.16, f32[2048]{0:T(1024)S(1)} %get-tuple-element.36), channel_id=1, replica_groups=mesh['tm_0'=4,'tm_1'=2,'tm_2'=8,'tm_3'=2,'chan'=2] {'tm_0'}, use_global_device_ids=true, to_apply=%region_0.1 | all-reduce | flops 4096 | bytes 32768 | tf_op jit(solution)/shard_map/psum | solution.py:57
  176.5 9.2 %all-reduce.3 = (f32[2048]{0:T(1024)S(1)}, f32[2048]{0:T(1024)S(1)}) all-reduce(f32[2048]{0:T(1024)S(1)} %get-tuple-element.7, f32[2048]{0:T(1024)S(1)} %get-tuple-element.8), channel_id=1, replica_groups=mesh['tm_0'=4,'tm_1'=2,'tm_2'=8,'tm_3'=2,'chan'=2] {'tm_1'}, use_global_device_ids=true, to_apply=%region_1.2 | all-reduce | flops 4096 | bytes 32768 | tf_op jit(solution)/shard_map/psum | solution.py:57
  185.7 20.9 %all-reduce = (f32[2048]{0:T(1024)S(1)}, f32[2048]{0:T(1024)S(1)}) all-reduce(f32[2048]{0:T(1024)S(1)} %get-tuple-element.11, f32[2048]{0:T(1024)S(1)} %get-tuple-element.12), channel_id=1, replica_groups=mesh['tm_0'=4,'tm_1'=2,'tm_2'=8,'tm_3'=2,'chan'=2] {'tm_2'}, use_global_device_ids=true, to_apply=%region_2.3 | all-reduce | flops 4096 | bytes 32768 | tf_op jit(solution)/shard_map/psum | solution.py:57
  206.7 26.6 %all-reduce.2 = (f32[2048]{0:T(1024)S(1)}, f32[2048]{0:T(1024)S(1)}) all-reduce(f32[2048]{0:T(1024)S(1)} %get-tuple-element.5, f32[2048]{0:T(1024)S(1)} %get-tuple-element.6), channel_id=1, replica_groups=mesh['tm_0'=4,'tm_1'=2,'tm_2'=8,'tm_3'=2,'chan'=2] {'tm_3'}, use_global_device_ids=true, to_apply=%region_3.4 | all-reduce | flops 4096 | bytes 32768 | tf_op jit(solution)/shard_map/psum | solution.py:57
  233.3 4.3 %multiply_add_fusion = f32[384,2048]{1,0:T(8,128)} fusion(f32[384,2048]{1,0:T(8,128)} %copy-done.6, f32[384,2048]{1,0:T(8,128)S(1)} %copy-done.5, f32[2048]{0:T(1024)S(1)} %multiply_add_fusion.1), kind=kLoop, calls=%fused_computation.15 | loop fusion | flops 1572864 | bytes 9445376 | tf_op jit(solution)/shard_map/add | solution.py:132
  (26 shorter events, 0.3 us)
Async XLA Ops:
  0.0 13.6 %copy-start.12 = (f32[384]{0:T(512)S(1)}, f32[384]{0:T(512)}, u32[]{:S(2)}) copy-start(f32[384]{0:T(512)} %param.7) | copy-start | bytes 4612
  0.0 14.2 %copy-start.11 = (f32[2048]{0:T(1024)S(1)}, f32[2048]{0:T(1024)}, u32[]{:S(2)}) copy-start(f32[2048]{0:T(1024)} %param.6) | copy-start | bytes 24580
  0.0 37.1 %collective-permute-start = (bf16[384,2048]{1,0:T(8,128)(2,1)}, bf16[384,2048]{1,0:T(8,128)(2,1)}, u32[]{:S(2)}, u32[]{:S(2)}) collective-permute-start(bf16[384,2048]{1,0:T(8,128)(2,1)} %param.4), channel_id=1, source_target_pairs={{0,2},{2,4},{4,6},{6,8},{8,10},{10,12},{12,14},{14,16},{16,18},{18... | collective-permute-start | bytes 4718600 | tf_op jit(solution)/shard_map/ppermute | solution.py:13
  17.1 1.7 copy-start.3
  27.9 4.0 %slice-start = ((s8[6291456]{0:T(1024)(128)(4,1)}), s8[4194304]{0:T(1024)(128)(4,1)S(1)}, s32[]{:S(2)}) async-start(s8[6291456]{0:T(1024)(128)(4,1)} %bitcast.30), calls=%async_computation | async-start | bytes 8388608
  28.0 4.6 %slice-start.1 = ((s8[6291456]{0:T(1024)(128)(4,1)}), s8[2097152]{0:T(1024)(128)(4,1)S(1)}, s32[]{:S(2)}) async-start(s8[6291456]{0:T(1024)(128)(4,1)} %bitcast.30), calls=%async_computation.1 | async-start | bytes 4194304
  32.6 1.7 copy-start.7
  33.4 6.2 %copy-start.1 = (f32[768,4096]{1,0:T(8,128)}, f32[768,4096]{1,0:T(8,128)S(1)}, u32[]{:S(2)}) copy-start(f32[768,4096]{1,0:T(8,128)S(1)} %constant_dynamic-update-slice_fusion) | copy-start | bytes 37748740
  34.3 5.3 %copy-start.8 = (bf16[384,2048]{1,0:T(8,128)(2,1)S(1)}, bf16[384,2048]{1,0:T(8,128)(2,1)}, u32[]{:S(2)}) copy-start(bf16[384,2048]{1,0:T(8,128)(2,1)} %param.4) | copy-start | bytes 4718596
  81.3 19.2 %copy-start = (f32[768,4096]{1,0:T(8,128)S(1)}, f32[768,4096]{1,0:T(8,128)}, u32[]{:S(2)}) copy-start(f32[768,4096]{1,0:T(8,128)} %get-tuple-element.29) | copy-start | bytes 37748740
  81.3 19.2 %copy-start.2 = (f32[768,1536]{1,0:T(8,128)S(1)}, f32[768,1536]{1,0:T(8,128)}, u32[]{:S(2)}) copy-start(f32[768,1536]{1,0:T(8,128)} %maximum_multiply_fusion) | copy-start | bytes 14155780
  100.5 17.2 %copy-start.4 = (f32[384,2048]{1,0:T(8,128)S(1)}, f32[384,2048]{1,0:T(8,128)}, u32[]{:S(2)}) copy-start(f32[384,2048]{1,0:T(8,128)} %copy-done.3) | copy-start | bytes 9437188
  100.5 17.2 %copy-start.9 = (f32[384]{0:T(512)S(1)}, f32[384]{0:T(512)}, u32[]{:S(2)}) copy-start(f32[384]{0:T(512)} %get-tuple-element.37) | copy-start | bytes 4612
  100.5 17.2 %copy-start.10 = (f32[384]{0:T(512)S(1)}, f32[384]{0:T(512)}, u32[]{:S(2)}) copy-start(f32[384]{0:T(512)} %get-tuple-element.38) | copy-start | bytes 4612
  117.7 115.6 %copy-start.5 = (f32[384,2048]{1,0:T(8,128)S(1)}, f32[384,2048]{1,0:T(8,128)}, u32[]{:S(2)}) copy-start(f32[384,2048]{1,0:T(8,128)} %copy-done.3) | copy-start | bytes 9437188
  124.2 1.7 copy-start.6
where the time goes:
time: 238 us
  blocking collectives  107 us (45%)
  matrix products  69.1 us (29%)
  other arithmetic  46.3 us (19%)
  local copies, waits for them, and re-layouts  12.2 us (5%)
  starting transfers between devices  3.02 us (1%)
    psum x4, blocking collectives, from_root(): array = lax.psum(array, axis)  69.6 us
    all_gather x4, blocking collectives, collected_together(): both, at, found = (lax.all_gather(jnp.concatenate(lines), axis), 0, {})  37.1 us
    dot_general x2, matrix products, invert(): jnp.dot(inverse[first:first + count], scaled, precision=lax.Precision.HIG...  36.4 us
    dot_general x1, matrix products, spectra(): jnp.dot(forward, segment.astype(jnp.float32), precision=lax.Precision.HIG...  23.3 us
    mul x1, other arithmetic, spectra(): spectrum * values[2 * length:]  18.3 us
    unnamed x31, local copies, waits for them, and re-layouts  11.3 us
    cos x1, other arithmetic, tables(): cosine = jnp.cos(angles)  10.5 us
    sin x1, other arithmetic, tables(): sine_table = jnp.sin(angles)  9.06 us
  transfers between devices with their start and end apart: 1, of which 0 were waited for; matrix products, arithmetic and copies ran while one was open for 13% of the time, Pallas kernels for 0%

commit v1 on v0

--- a/solution.py
+++ b/solution.py
@@ -54,7 +54,7 @@
 def from_root(array, axes, root):
     array = jnp.where(lax.axis_index(axes) == root, array, jnp.zeros_like(array))
     for axis in axes:
-        array = lax.psum(array, axis)
+        array = jnp.sum(lax.all_gather(array, axis_name=axis), 0)
     return array
 
 

time: 238 us -> 265 us (1.11)
  blocking collectives: 107 us -> 135 us
    all_gather x0 -> x8, blocking collectives: none -> 98.4 us  [from_root(): array = jnp.sum(lax.all_gather(array, axis_name=axis), 0)]
    psum x4 -> x0, blocking collectives: 69.6 us -> none  [from_root(): array = lax.psum(array, axis)]
  transfers between devices with their start and end apart: 1 -> 1, of which waited for: 0 -> 0; matrix products, arithmetic and copies ran while one was open for 13% -> 11% of each run, Pallas kernels for 0% -> 0%
where the time goes in v1:
time: 265 us
  blocking collectives  135 us (51%)
  matrix products  69.1 us (26%)
  other arithmetic  46.6 us (18%)
  local copies, waits for them, and re-layouts  10.6 us (4%)
  starting transfers between devices  3.02 us (1%)
    all_gather x8, blocking collectives, from_root(): array = jnp.sum(lax.all_gather(array, axis_name=axis), 0)  98.4 us
    all_gather x4, blocking collectives, collected_together(): both, at, found = (lax.all_gather(jnp.concatenate(lines), axis), 0, {})  37.1 us
    dot_general x2, matrix products, invert(): jnp.dot(inverse[first:first + count], scaled, precision=lax.Precision.HIG...  36.4 us
    dot_general x1, matrix products, spectra(): jnp.dot(forward, segment.astype(jnp.float32), precision=lax.Precision.HIG...  23.3 us
    mul x1, other arithmetic, spectra(): spectrum * values[2 * length:]  18.3 us
    cos x1, other arithmetic, tables(): cosine = jnp.cos(angles)  10.5 us
    unnamed x31, local copies, waits for them, and re-layouts  9.67 us
    sin x1, other arithmetic, tables(): sine_table = jnp.sin(angles)  9.06 us
  transfers between devices with their start and end apart: 1, of which 0 were waited for; matrix products, arithmetic and copies ran while one was open for 11% of the time, Pallas kernels for 0%

profile of v1, /device:TPU:1, one launch (start us, length us, event | category | flops | bytes accessed | tf_op | source)
XLA Modules:
  0.0 265.2 jit_solution(4006991591550160351)
XLA Ops:
  0.0 3.0 %collective-permute-start = (bf16[384,2048]{1,0:T(8,128)(2,1)}, bf16[384,2048]{1,0:T(8,128)(2,1)}, u32[]{:S(2)}, u32[]{:S(2)}) collective-permute-start(bf16[384,2048]{1,0:T(8,128)(2,1)} %param.4), channel_id=1, source_target_pairs={{0,2},{2,4},{4,6},{6,8},{8,10},{10,12},{12,14},{14,16},{16,18},{18... | collective-permute-start | bytes 4718600 | tf_op jit(solution)/shard_map/ppermute | solution.py:13
  3.0 10.5 %fusion.32 = (f32[768,768]{1,0:T(8,128)S(1)}, f32[768,768]{1,0:T(8,128)}) fusion(), kind=kLoop, calls=%fused_computation.39 | loop fusion | flops 5898240 | bytes 4718592 | tf_op jit(solution)/shard_map/cos | solution.py:69
  13.5 0.1 slice.241
  13.6 0.0 copy-done.12
  13.6 0.6 broadcast_subtract_fusion
  14.2 0.0 copy-done.11
  14.2 2.9 %fusion.18 = f32[384,2048]{1,0:T(8,128)S(1)} fusion(f32[2048]{0:T(1024)S(1)} %copy-done.11, f32[384]{0:T(512)S(1)} %get-tuple-element.36), kind=kOutput, calls=%fused_computation.25 | convolution fusion | flops 3624812544 | bytes 3155456 | tf_op jit(solution)/shard_map/dot_general | solution.py:115
  17.1 0.0 copy-start.3
  17.1 1.7 copy-done.3
  18.8 9.1 %fusion.31 = f32[768,768]{1,0:T(8,128)S(1)} fusion(), kind=kLoop, calls=%fused_computation.38 | loop fusion | flops 5308416 | bytes 2359296 | tf_op jit(solution)/shard_map/sin | solution.py:70
  27.9 0.0 slice-start
  27.9 0.1 slice_negate_fusion
  28.0 0.0 slice-start.1
  28.0 3.4 %constant_dynamic-update-slice_fusion.1 = f32[768,4096]{1,0:T(8,128)S(1)} fusion(f32[768,2048]{1,0:T(8,128)} %param.5), kind=kLoop, calls=%fused_computation.129 | loop fusion | bytes 12582912
  31.4 0.5 slice-done
  31.9 0.7 slice-done.1
  32.6 0.8 constant_dynamic-update-slice_fusion
  33.4 0.0 copy-start.1
  33.4 0.9 copy-done.7
  34.3 2.8 %maximum_multiply_fusion = f32[768,1536]{1,0:T(8,128)} fusion(f32[768,768]{1,0:T(8,128)S(1)} %copy-done.7, f32[768,768]{1,0:T(8,128)S(1)} %get-tuple-element.37), kind=kLoop, calls=%fused_computation.9 | loop fusion | flops 2359296 | bytes 9437184 | tf_op jit(solution)/shard_map/div | solution.py:72
  37.1 0.0 collective-permute-done
  37.1 2.5 copy-done.1
  39.6 0.0 copy-done.8
  39.6 23.3 %fusion.5 = f32[1536,4096]{1,0:T(8,128)} fusion(bf16[384,2048]{1,0:T(8,128)(2,1)} %collective-permute-done, bf16[384,2048]{1,0:T(8,128)(2,1)S(1)} %copy-done.8, f32[768,384]{1,0:T(8,128)S(1)} %slice_negate_fusion, f32[768,384]{1,0:T(8,128)S(1)} %slice.241), kind=kOutput, calls=%fused_computation.11 | convolution fusion | flops 28997910528 | bytes 30670848 | tf_op jit(solution)/shard_map/dot_general | solution.py:77
  62.9 18.3 %slice_multiply_fusion = (f32[768,4096]{1,0:T(8,128)S(1)}, f32[768,4096]{1,0:T(8,128)}) fusion(f32[768,4096]{1,0:T(8,128)} %copy-done.1, f32[1536,4096]{1,0:T(8,128)} %fusion.5), kind=kLoop, calls=%fused_computation.7 | loop fusion | flops 6291456 | bytes 62914560 | tf_op jit(solution)/shard_map/mul | solution.py:84
  81.2 19.2 %fusion.3 = f32[384,2048]{1,0:T(8,128)} fusion(f32[768,4096]{1,0:T(8,128)S(1)} %get-tuple-element.26, f32[768,4096]{1,0:T(8,128)} %get-tuple-element.27, f32[768,1536]{1,0:T(8,128)} %maximum_multiply_fusion), kind=kOutput, calls=%fused_computation.5 | convolution fusion | flops 14498660352 | bytes 30670848 | tf_op jit(solution)/shard_map/dot_general | solution.py:89
  100.4 0.0 copy-done
  100.5 17.2 %fusion.1 = f32[384,2048]{1,0:T(8,128)} fusion(f32[768,4096]{1,0:T(8,128)S(1)} %copy-done, f32[768,4096]{1,0:T(8,128)S(1)} %get-tuple-element.26, f32[768,1536]{1,0:T(8,128)S(1)} %copy-done.2), kind=kOutput, calls=%fused_computation.3 | convolution fusion | flops 14498660352 | bytes 30670848 | tf_op jit(solution)/shard_map/dot_general | solution.py:89
  117.6 0.0 copy-done.9
  117.6 0.0 copy-start.5
  117.7 6.5 %exponential_multiply_fusion = f32[384,2048]{1,0:T(8,128)S(1)} fusion(f32[384,2048]{1,0:T(8,128)S(1)} %copy-done.4, f32[384,2048]{1,0:T(8,128)} %fusion.1, f32[384,2048]{1,0:T(8,128)} %fusion.3, f32[2048]{0:T(1024)S(1)} %exponential-minus-one_negate_fusion, f32[384]{0:T(512)S(1)} %copy-done.10, f32[384]{0:T(512)S(1)} %copy-done.9), kind=kOutput, calls=%fused_computation.27 | convolution fusion | flops 3629531136 | bytes 12594176 | tf_op jit(solution)/shard_map/dot_general | solution.py:119
  124.2 0.0 copy-start.6
  124.3 1.8 all-gather.10
  126.2 21.2 %all-gather.11 = f32[8,2,2048]{2,1,0:T(2,128)S(1)} all-gather(f32[1,2,2048]{2,1,0:T(2,128)S(1)} %maximum_bitcast_fusion.1), channel_id=3, replica_groups=mesh['tm_0'=4,'tm_1'=2,'tm_2'=8,'tm_3'=2,'chan'=2] {'tm_2'}, dimensions={0}, use_global_device_ids=true | all-gather | bytes 147456 | tf_op jit(solution)/shard_map/all_gather | solution.py:30
  147.4 0.1 bitcast_add_fusion.1
  147.6 4.8 %all-gather.12 = f32[2,2,2048]{2,1,0:T(2,128)S(1)} all-gather(f32[1,2,2048]{2,1,0:T(2,128)S(1)} %maximum_bitcast_fusion.2), channel_id=4, replica_groups=mesh['tm_0'=4,'tm_1'=2,'tm_2'=8,'tm_3'=2,'chan'=2] {'tm_1'}, dimensions={0}, use_global_device_ids=true | all-gather | bytes 49152 | tf_op jit(solution)/shard_map/all_gather | solution.py:30
  152.4 9.3 %all-gather.13 = f32[4,2,2048]{2,1,0:T(2,128)S(1)} all-gather(f32[1,2,2048]{2,1,0:T(2,128)S(1)} %maximum_bitcast_fusion.3), channel_id=5, replica_groups=mesh['tm_0'=4,'tm_1'=2,'tm_2'=8,'tm_3'=2,'chan'=2] {'tm_0'}, dimensions={0}, use_global_device_ids=true | all-gather | bytes 81920 | tf_op jit(solution)/shard_map/all_gather | solution.py:30
  161.7 0.1 fusion.43
  161.8 0.3 fusion.42
  162.1 9.0 %all-gather.14 = f32[4,1,2048]{2,1,0:T(1,128)S(1)} all-gather(f32[1,1,2048]{2,1,0:T(1,128)S(1)} %get-tuple-element.9), channel_id=1, replica_groups=mesh['tm_0'=4,'tm_1'=2,'tm_2'=8,'tm_3'=2,'chan'=2] {'tm_0'}, dimensions={0}, use_global_device_ids=true | all-gather | bytes 40960 | tf_op jit(solution)/shard_map/all_gather | solution.py:57
  171.2 4.7 %all-gather.4 = f32[4096]{0:T(1024)S(1)} all-gather(f32[2048]{0:T(1024)S(1)} %reduce_sum.72), channel_id=6, replica_groups=mesh['tm_0'=4,'tm_1'=2,'tm_2'=8,'tm_3'=2,'chan'=2] {'tm_1'}, dimensions={0}, use_global_device_ids=true | all-gather | bytes 24576 | tf_op jit(solution)/shard_map/all_gather | solution.py:57
  175.9 18.5 %all-gather.5 = f32[16384]{0:T(1024)S(1)} all-gather(f32[2048]{0:T(1024)S(1)} %reduce_sum.73), channel_id=7, replica_groups=mesh['tm_0'=4,'tm_1'=2,'tm_2'=8,'tm_3'=2,'chan'=2] {'tm_2'}, dimensions={0}, use_global_device_ids=true | all-gather | bytes 73728 | tf_op jit(solution)/shard_map/all_gather | solution.py:57
  194.5 21.9 %all-gather.6 = f32[4096]{0:T(1024)S(1)} all-gather(f32[2048]{0:T(1024)S(1)} %reduce_sum.74), channel_id=8, replica_groups=mesh['tm_0'=4,'tm_1'=2,'tm_2'=8,'tm_3'=2,'chan'=2] {'tm_3'}, dimensions={0}, use_global_device_ids=true | all-gather | bytes 24576 | tf_op jit(solution)/shard_map/all_gather | solution.py:57
  216.4 9.0 %all-gather.15 = f32[4,1,2048]{2,1,0:T(1,128)S(1)} all-gather(f32[1,1,2048]{2,1,0:T(1,128)S(1)} %get-tuple-element.5), channel_id=1, replica_groups=mesh['tm_0'=4,'tm_1'=2,'tm_2'=8,'tm_3'=2,'chan'=2] {'tm_0'}, dimensions={0}, use_global_device_ids=true | all-gather | bytes 40960 | tf_op jit(solution)/shard_map/all_gather | solution.py:57
  225.5 4.7 %all-gather.7 = f32[4096]{0:T(1024)S(1)} all-gather(f32[2048]{0:T(1024)S(1)} %reduce_sum.76), channel_id=9, replica_groups=mesh['tm_0'=4,'tm_1'=2,'tm_2'=8,'tm_3'=2,'chan'=2] {'tm_1'}, dimensions={0}, use_global_device_ids=true | all-gather | bytes 24576 | tf_op jit(solution)/shard_map/all_gather | solution.py:57
  230.3 18.2 %all-gather.8 = f32[16384]{0:T(1024)S(1)} all-gather(f32[2048]{0:T(1024)S(1)} %reduce_sum.77), channel_id=10, replica_groups=mesh['tm_0'=4,'tm_1'=2,'tm_2'=8,'tm_3'=2,'chan'=2] {'tm_2'}, dimensions={0}, use_global_device_ids=true | all-gather | bytes 73728 | tf_op jit(solution)/shard_map/all_gather | solution.py:57
  248.5 12.2 %all-gather.9 = f32[4096]{0:T(1024)S(1)} all-gather(f32[2048]{0:T(1024)S(1)} %reduce_sum.78), channel_id=11, replica_groups=mesh['tm_0'=4,'tm_1'=2,'tm_2'=8,'tm_3'=2,'chan'=2] {'tm_3'}, dimensions={0}, use_global_device_ids=true | all-gather | bytes 24576 | tf_op jit(solution)/shard_map/all_gather | solution.py:57
  261.0 4.3 %multiply_add_fusion = f32[384,2048]{1,0:T(8,128)} fusion(f32[384,2048]{1,0:T(8,128)} %copy-done.6, f32[384,2048]{1,0:T(8,128)S(1)} %copy-done.5, f32[2048]{0:T(1024)S(1)} %add_add_fusion), kind=kLoop, calls=%fused_computation.15 | loop fusion | flops 1572864 | bytes 9445376 | tf_op jit(solution)/shard_map/add | solution.py:132
  (43 shorter events, 0.7 us)
Async XLA Ops:
  0.0 13.6 %copy-start.12 = (f32[384]{0:T(512)S(1)}, f32[384]{0:T(512)}, u32[]{:S(2)}) copy-start(f32[384]{0:T(512)} %param.7) | copy-start | bytes 4612
  0.0 14.2 %copy-start.11 = (f32[2048]{0:T(1024)S(1)}, f32[2048]{0:T(1024)}, u32[]{:S(2)}) copy-start(f32[2048]{0:T(1024)} %param.6) | copy-start | bytes 24580
  0.0 37.1 %collective-permute-start = (bf16[384,2048]{1,0:T(8,128)(2,1)}, bf16[384,2048]{1,0:T(8,128)(2,1)}, u32[]{:S(2)}, u32[]{:S(2)}) collective-permute-start(bf16[384,2048]{1,0:T(8,128)(2,1)} %param.4), channel_id=1, source_target_pairs={{0,2},{2,4},{4,6},{6,8},{8,10},{10,12},{12,14},{14,16},{16,18},{18... | collective-permute-start | bytes 4718600 | tf_op jit(solution)/shard_map/ppermute | solution.py:13
  17.1 1.7 copy-start.3
  27.9 4.0 %slice-start = ((s8[6291456]{0:T(1024)(128)(4,1)}), s8[4194304]{0:T(1024)(128)(4,1)S(1)}, s32[]{:S(2)}) async-start(s8[6291456]{0:T(1024)(128)(4,1)} %bitcast.86), calls=%async_computation | async-start | bytes 8388608
  28.0 4.6 %slice-start.1 = ((s8[6291456]{0:T(1024)(128)(4,1)}), s8[2097152]{0:T(1024)(128)(4,1)S(1)}, s32[]{:S(2)}) async-start(s8[6291456]{0:T(1024)(128)(4,1)} %bitcast.86), calls=%async_computation.1 | async-start | bytes 4194304
  32.6 1.7 copy-start.7
  33.4 6.2 %copy-start.1 = (f32[768,4096]{1,0:T(8,128)}, f32[768,4096]{1,0:T(8,128)S(1)}, u32[]{:S(2)}) copy-start(f32[768,4096]{1,0:T(8,128)S(1)} %constant_dynamic-update-slice_fusion) | copy-start | bytes 37748740
  34.3 5.3 %copy-start.8 = (bf16[384,2048]{1,0:T(8,128)(2,1)S(1)}, bf16[384,2048]{1,0:T(8,128)(2,1)}, u32[]{:S(2)}) copy-start(bf16[384,2048]{1,0:T(8,128)(2,1)} %param.4) | copy-start | bytes 4718596
  81.2 19.2 %copy-start = (f32[768,4096]{1,0:T(8,128)S(1)}, f32[768,4096]{1,0:T(8,128)}, u32[]{:S(2)}) copy-start(f32[768,4096]{1,0:T(8,128)} %get-tuple-element.27) | copy-start | bytes 37748740
  81.2 19.2 %copy-start.2 = (f32[768,1536]{1,0:T(8,128)S(1)}, f32[768,1536]{1,0:T(8,128)}, u32[]{:S(2)}) copy-start(f32[768,1536]{1,0:T(8,128)} %maximum_multiply_fusion) | copy-start | bytes 14155780
  100.4 17.2 %copy-start.4 = (f32[384,2048]{1,0:T(8,128)S(1)}, f32[384,2048]{1,0:T(8,128)}, u32[]{:S(2)}) copy-start(f32[384,2048]{1,0:T(8,128)} %copy-done.3) | copy-start | bytes 9437188
  100.4 17.2 %copy-start.9 = (f32[384]{0:T(512)S(1)}, f32[384]{0:T(512)}, u32[]{:S(2)}) copy-start(f32[384]{0:T(512)} %get-tuple-element.34) | copy-start | bytes 4612
  100.4 17.2 %copy-start.10 = (f32[384]{0:T(512)S(1)}, f32[384]{0:T(512)}, u32[]{:S(2)}) copy-start(f32[384]{0:T(512)} %get-tuple-element.35) | copy-start | bytes 4612
  117.6 143.3 %copy-start.5 = (f32[384,2048]{1,0:T(8,128)S(1)}, f32[384,2048]{1,0:T(8,128)}, u32[]{:S(2)}) copy-start(f32[384,2048]{1,0:T(8,128)} %copy-done.3) | copy-start | bytes 9437188
  124.2 37.9 %copy-start.6 = (f32[384,2048]{1,0:T(8,128)}, f32[384,2048]{1,0:T(8,128)S(1)}, u32[]{:S(2)}) copy-start(f32[384,2048]{1,0:T(8,128)S(1)} %exponential_multiply_fusion) | copy-start | bytes 9437188
